TPU v7x, 32 devices: a whole 2x2x4 slice. The times are simulated.
32 devices in a mesh: dp: 8 (over z, core), tp: 4 (over y, x).
Axes of the slice: x: 2, y: 2, z: 4, core: 2. Of those that a mesh axis runs over, the one named last changes fastest.
Arguments:
- hidden: bfloat16 [384, 4096], P('dp'), may hold values from -6 to 6
- w_qkv: bfloat16 [4096, 4608], P('dp', 'tp'), may hold values from -0.09375 to 0.09375
- w_out: bfloat16 [4096, 4096], P('tp', 'dp'), may hold values from -0.125 to 0.125
- norm_gain: float32 [4096], replicated, may hold values from 0.5 to 1.5
- kv_cache: bfloat16 [384, 2, 128, 256], P(('dp', 'tp')), may hold values from -110 to 110
- lengths: int32 [384], P(('dp', 'tp')), may hold values from 1 to 127, as said below
Outputs:
- residual_out: bfloat16 [384, 4096], P('dp', 'tp')
- scaled: bfloat16 [384, 4096], P('dp', 'tp')
- row_scale: float32 [384], P('dp')
Inputs may be any that keep to these rules, and one draw needn't show every extreme that they name: `lengths`: every sequence has 1 to 127 live positions; among each device's 12 sequences one has exactly 127.
All inputs are finite; a program needn't handle non-finite values.
Results may differ from a plain program's by a relative error of at most 0.015.
Values may be sent and summed in bfloat16 or wider, within the bound.
A program may use at most 64 MiB of HBM per device.

v0:
```python
import functools

import jax
import jax.numpy as jnp
from jax import lax
from jax.experimental import pallas as pl
from jax.experimental.pallas import tpu as pltpu
from jax.sharding import PartitionSpec as P


def rope(values, positions):
    half = values.shape[-1] // 2
    freqs = 1000000.0 ** (-2.0 * jnp.arange(half, dtype=jnp.float32) / values.shape[-1])
    angle = positions[..., None] * freqs
    cosine = jnp.cos(angle)
    sine = jnp.sin(angle)
    first = values[..., :half]
    second = values[..., half:]
    return jnp.concatenate(
        [first * cosine - second * sine, second * cosine + first * sine], axis=-1
    )


def shards(hidden, w_qkv, w_out, norm_gain, kv_cache, lengths):
    seq_dev = kv_cache.shape[0]
    kv_heads = kv_cache.shape[1]
    head_size = kv_cache.shape[3] // 2
    tp_count = lax.axis_size("tp")
    w_cols = lax.all_gather(w_qkv, "dp", axis=0, tiled=True)
    qkv_part = jnp.dot(hidden, w_cols, preferred_element_type=jnp.float32)
    mine = lax.all_to_all(
        qkv_part.astype(jnp.bfloat16), "tp", split_axis=0, concat_axis=1, tiled=True
    )
    att_width = w_out.shape[0] * tp_count
    heads = att_width // head_size
    groups = heads // kv_heads
    positions = lengths.astype(jnp.float32)[:, None]
    query = rope(
        mine[:, :att_width].reshape(seq_dev, heads, head_size).astype(jnp.float32), positions
    ).astype(jnp.bfloat16)
    key_new = rope(
        mine[:, att_width : att_width + kv_heads * head_size]
        .reshape(seq_dev, kv_heads, head_size)
        .astype(jnp.float32),
        positions,
    ).astype(jnp.bfloat16)
    value_new = mine[:, att_width + kv_heads * head_size :].reshape(seq_dev, kv_heads, head_size)
    q_grp = query.reshape(seq_dev, kv_heads, groups, head_size)
    keys = kv_cache[..., :head_size]
    vals = kv_cache[..., head_size:]
    scale = 1.0 / head_size**0.5
    scores = jnp.einsum("nkgd,nkpd->nkgp", q_grp, keys, preferred_element_type=jnp.float32) * scale
    own = jnp.einsum("nkgd,nkd->nkg", q_grp, key_new, preferred_element_type=jnp.float32) * scale
    valid = (jnp.arange(kv_cache.shape[2])[None, :] < lengths[:, None])[:, None, None, :]
    scores = jnp.where(valid, scores, jnp.float32(-1e30))
    top = jnp.maximum(jnp.max(scores, axis=-1), own)
    probs = jnp.where(valid, jnp.exp(scores - top[..., None]), jnp.float32(0.0))
    own_prob = jnp.exp(own - top)
    denom = jnp.sum(probs, axis=-1) + own_prob
    weights = (probs / denom[..., None]).astype(jnp.bfloat16)
    own_weight = (own_prob / denom).astype(jnp.bfloat16)
    mixed = jnp.einsum("nkgp,nkpd->nkgd", weights, vals, preferred_element_type=jnp.float32)
    mixed = (
        mixed
        + own_weight.astype(jnp.float32)[..., None] * value_new.astype(jnp.float32)[:, :, None, :]
    )
    attn = mixed.reshape(seq_dev, att_width).astype(jnp.bfloat16)
    heads_part = lax.all_to_all(attn, "tp", split_axis=1, concat_axis=0, tiled=True)
    terms = jnp.dot(
        heads_part,
        lax.all_gather(w_out, "dp", axis=1, tiled=True),
        preferred_element_type=jnp.float32,
    )
    width = terms.shape[1]
    share = width // tp_count
    offset = lax.axis_index("tp") * share
    summed = lax.psum_scatter(
        terms.astype(jnp.bfloat16), "tp", scatter_dimension=1, tiled=True
    ).astype(jnp.float32)
    hidden_mine = lax.dynamic_slice_in_dim(hidden, offset, share, 1).astype(jnp.float32)
    gain_mine = lax.dynamic_slice_in_dim(norm_gain, offset, share, 0)
    resid_mine = hidden_mine + summed
    weighted = resid_mine * gain_mine[None, :]
    squares = lax.psum(jnp.sum(resid_mine * resid_mine, axis=-1), "tp")
    peak = lax.pmax(jnp.max(jnp.abs(weighted), axis=-1), "tp")
    inverse = lax.rsqrt(squares / width + 1e-06)
    normed_mine = weighted * inverse[:, None]
    row_scale = (peak * inverse + 1e-06) / 448.0
    residual_out = resid_mine.astype(jnp.bfloat16)
    scaled = (normed_mine / row_scale[:, None]).astype(jnp.bfloat16)
    return (residual_out, scaled, row_scale)


F32 = jnp.float32
BF16 = jnp.bfloat16
MESH = pl.DeviceIdType.MESH


def send(src, dst, send_sem, recv_sem, where):
    copy = pltpu.make_async_remote_copy(
        src_ref=src, dst_ref=dst, send_sem=send_sem, recv_sem=recv_sem,
        device_id=where, device_id_type=MESH,
    )
    copy.start()
    return copy


def layer(
    n_dp, n_tp,
    hidden, w_qkv, w_out, gain, cache, lens,
    resid_out, scaled_out, scale_out,
    h_all, w1, w2, kv, hid, hid32, p_send, p_recv, r_acc, r_send, r_recv, mine32,
    t1_send, t1_recv, q_rows, k_rows, v_rows, l_rows, s_rows, a_rows,
    t2_send, t2_recv, b_rows, ag, mm, mq, t3_send, t3_recv, f_send, f_recv,
    o_send, o_recv, c_send, c_recv, fin,
    loc_sem, h_s, h_r, p_s, p_r, r_s, r_r, t1_s, t1_r, t2_s, t2_r,
    g_s, g_r, x_s, t3_s, t3_r, f_s, f_r, o_s, o_r, c_s, c_r,
):
    dp = lax.axis_index("dp")
    tp = lax.axis_index("tp")
    core = lax.rem(dp, 2)
    chip = dp // 2
    other = 1 - core
    partner = chip * 2 + other
    n_chip = n_dp // 2
    rows = hidden.shape[0]
    seqs = rows // n_tp
    depth = w_qkv.shape[0]
    ocols = w_out.shape[1]
    owide = resid_out.shape[1]
    kvh = cache.shape[1]
    ctx = cache.shape[2]
    hd = cache.shape[3] // 2
    heads = (w_out.shape[0] * n_tp) // hd
    groups = heads // kvh
    per = w_qkv.shape[1] // hd
    per_out = w_out.shape[0] // hd
    width = hidden.shape[1]

    load_hid = pltpu.make_async_copy(hidden, hid, loc_sem.at[4])
    load_hid.start()
    own_h = pltpu.make_async_copy(
        hidden.at[:, pl.ds(pl.multiple_of(dp * depth, depth), depth)], h_all.at[core, chip], loc_sem.at[0])
    own_h.start()
    load_w1 = pltpu.make_async_copy(w_qkv, w1, loc_sem.at[1])
    load_w1.start()

    barrier = pltpu.get_barrier_semaphore()
    for d in range(1, n_dp):
        pl.semaphore_signal(barrier, inc=1, device_id={"dp": lax.rem(dp + d, n_dp)}, device_id_type=MESH)
    for d in range(1, n_tp):
        pl.semaphore_signal(barrier, inc=1, device_id={"tp": lax.rem(tp + d, n_tp)}, device_id_type=MESH)
    pl.semaphore_wait(barrier, n_dp + n_tp - 2)

    load_hid.wait()
    pending = []
    for d in [*range(1, n_dp, 2), *range(2, n_dp, 2)]:
        peer = lax.rem(dp + d, n_dp)
        pending.append(send(
            hid.at[:, pl.ds(pl.multiple_of(peer * depth, depth), depth)],
            h_all.at[core, chip], h_s.at[peer], h_r.at[dp], {"dp": peer}))
    load_kv = pltpu.make_async_copy(cache, kv, loc_sem.at[2])
    load_kv.start()
    load_w2 = pltpu.make_async_copy(w_out, w2, loc_sem.at[3])
    load_w2.start()

    row_i = lax.broadcasted_iota(jnp.int32, (seqs, hd), 0)
    lane_i = lax.broadcasted_iota(jnp.int32, (seqs, hd), 1)
    live = jnp.zeros((seqs, hd), jnp.int32)
    for n in range(seqs):
        live = jnp.where(row_i == n, lens[n], live)
    half = hd // 2
    low = lane_i < half
    index = jnp.where(low, lane_i, lane_i - half).astype(F32)
    freqs = jnp.exp(index * F32(-2.0 * 13.815510557964274 / hd))
    angle = live.astype(F32) * freqs
    cosine = jnp.cos(angle)
    sine = jnp.where(low, -jnp.sin(angle), jnp.sin(angle))
    for h in range(heads):
        l_rows[pl.ds(h, seqs, stride=heads), :] = live.astype(F32)
    hid32[...] = hid[...].astype(F32)
    for r in range(n_dp):
        block = slice(r * ocols, (r + 1) * ocols)
        mine = hid32[0:seqs, block]
        for q in range(1, n_tp):
            mine = jnp.where(tp == q, hid32[q * seqs : (q + 1) * seqs, block], mine)
        fin[:, block] = mine

    def recv_h(peer):
        pltpu.make_async_remote_copy(
            src_ref=h_all.at[core, chip], dst_ref=h_all.at[lax.rem(peer, 2), peer // 2],
            send_sem=h_s.at[peer], recv_sem=h_r.at[peer],
            device_id={"dp": peer}, device_id_type=MESH).wait_recv()

    own_h.wait()
    load_w1.wait()
    for d in range(n_chip):
        recv_h(2 * d + other)
    part = jnp.dot(h_all[other].reshape(n_chip * rows, depth), w1[...], preferred_element_type=F32)
    p_send[...] = part.astype(BF16).reshape(p_send.shape)
    swap = send(p_send, p_recv, p_s, p_r, {"dp": partner})
    pending.append(swap)
    for d in range(1, n_chip):
        recv_h(2 * lax.rem(chip + d, n_chip) + core)
    part = jnp.dot(h_all[core].reshape(n_chip * rows, depth), w1[...], preferred_element_type=F32)
    r_acc[...] = part.reshape(r_acc.shape)
    swap.wait_recv()
    for d in range(1, n_chip):
        to = lax.rem(chip + d, n_chip)
        r_send[to] = (r_acc[to] + p_recv[to].astype(F32)).astype(BF16)
        pending.append(send(r_send.at[to], r_recv.at[chip], r_s.at[to], r_r.at[chip], {"dp": to * 2 + core}))
    total = r_acc[chip] + p_recv[chip].astype(F32)
    for d in range(1, n_chip):
        who = lax.rem(chip + d, n_chip)
        pltpu.make_async_remote_copy(
            src_ref=r_send.at[who], dst_ref=r_recv.at[who], send_sem=r_s.at[who], recv_sem=r_r.at[who],
            device_id={"dp": who * 2 + core}, device_id_type=MESH).wait_recv()
        total = total + r_recv[who].astype(F32)
    mine32[...] = total

    def exchange(src, dst, s_sem, r_sem, fill):
        for q in range(n_tp):
            fill(q)
        keep = pltpu.make_async_copy(src.at[tp], dst.at[tp], r_sem.at[tp])
        keep.start()
        sent = []
        for d in range(1, n_tp):
            peer = lax.rem(tp + d, n_tp)
            sent.append(send(src.at[peer], dst.at[tp], s_sem.at[peer], r_sem.at[tp], {"tp": peer}))
        keep.wait()
        for d in range(1, n_tp):
            peer = lax.rem(tp + d, n_tp)
            pltpu.make_async_remote_copy(
                src_ref=src.at[peer], dst_ref=dst.at[peer], send_sem=s_sem.at[peer], recv_sem=r_sem.at[peer],
                device_id={"tp": peer}, device_id_type=MESH).wait_recv()
        return sent

    def fill1(q):
        t1_send[q] = mine32[q * seqs : (q + 1) * seqs, :].astype(BF16)

    pending += exchange(t1_send, t1_recv, t1_s, t1_r, fill1)

    def head(h):
        return t1_recv[h // per, :, (h % per) * hd : (h % per + 1) * hd].astype(F32)

    def turn(x):
        return (x * cosine + pltpu.roll(x, half, 1) * sine).astype(BF16).astype(F32)

    for h in range(heads):
        q_rows[pl.ds(h, seqs, stride=heads), :] = turn(head(h))
    for k in range(kvh):
        key_new = turn(head(heads + k))
        value_new = head(heads + kvh + k)
        for g in range(groups):
            k_rows[pl.ds(k * groups + g, seqs, stride=heads), :] = key_new
            v_rows[pl.ds(k * groups + g, seqs, stride=heads), :] = value_new
    load_kv.wait()
    for n in range(seqs):
        for k in range(kvh):
            at = (n * kvh + k) * groups
            s_rows[at : at + groups, :] = lax.dot_general(
                q_rows[at : at + groups, :].astype(BF16), kv[n, k, :, :hd],
                (((1,), (1,)), ((), ())), preferred_element_type=F32)
    factor = F32(1.0 / hd**0.5)
    pos = lax.broadcasted_iota(jnp.int32, (seqs * heads, ctx), 1).astype(F32)
    valid = pos < l_rows[...]
    scores = jnp.where(valid, s_rows[...] * factor, F32(-1e30))
    own = jnp.sum(q_rows[...] * k_rows[...], axis=1, keepdims=True) * factor
    top = jnp.maximum(jnp.max(scores, axis=1, keepdims=True), own)
    probs = jnp.where(valid, jnp.exp(scores - top), F32(0.0))
    own_prob = jnp.exp(own - top)
    denom = jnp.sum(probs, axis=1, keepdims=True) + own_prob
    s_rows[...] = probs / denom
    own_weight = (own_prob / denom).astype(BF16).astype(F32)
    v_rows[...] = own_weight * v_rows[...]
    for n in range(seqs):
        for k in range(kvh):
            at = (n * kvh + k) * groups
            a_rows[at : at + groups, :] = jnp.dot(
                s_rows[at : at + groups, :].astype(BF16), kv[n, k, :, hd:],
                preferred_element_type=F32) + v_rows[at : at + groups, :]

    def fill2(q):
        for e in range(per_out):
            t2_send[q, :, e * hd : (e + 1) * hd] = a_rows[
                pl.ds(q * per_out + e, seqs, stride=heads), :].astype(BF16)

    pending += exchange(t2_send, t2_recv, t2_s, t2_r, fill2)
    for q in range(n_tp):
        b_rows[q * seqs : (q + 1) * seqs, :] = t2_recv[q].astype(F32)
    ag[core, chip] = b_rows[...].astype(BF16)
    for d in range(1, n_chip):
        to = lax.rem(chip + d, n_chip)
        pending.append(send(ag.at[core, chip], ag.at[core, chip], g_s.at[to], g_r.at[core, chip],
                            {"dp": to * 2 + core}))
    pending.append(send(ag.at[core, chip], ag.at[core, chip], x_s.at[chip], g_r.at[core, chip], {"dp": partner}))

    def recv_g(c, who):
        pltpu.make_async_remote_copy(
            src_ref=ag.at[core, chip], dst_ref=ag.at[c, who], send_sem=x_s.at[chip], recv_sem=g_r.at[c, who],
            device_id={"dp": partner}, device_id_type=MESH).wait_recv()

    for d in range(1, n_chip):
        who = lax.rem(chip + d, n_chip)
        recv_g(core, who)
        pending.append(send(ag.at[core, who], ag.at[core, who], x_s.at[who], g_r.at[core, who], {"dp": partner}))
    load_w2.wait()
    def project(side):
        mm[side] = jnp.dot(ag[side].reshape(n_chip * rows, w_out.shape[0]), w2[...],
                           preferred_element_type=F32).reshape(n_chip, rows, ocols)
        for q in range(n_tp):
            for c in range(n_chip):
                mq[q, side, c * seqs : (c + 1) * seqs, :] = mm[side, c, q * seqs : (q + 1) * seqs, :]
            t3_send[q, side] = mq[q, side].astype(BF16)
        for d in range(1, n_tp):
            peer = lax.rem(tp + d, n_tp)
            pending.append(send(
                t3_send.at[peer, side], t3_recv.at[tp, side], t3_s.at[peer, side], t3_r.at[tp, side],
                {"tp": peer}))

    def scatter(side):
        total = t3_send[tp, side].astype(F32)
        for d in range(1, n_tp):
            peer = lax.rem(tp + d, n_tp)
            pltpu.make_async_remote_copy(
                src_ref=t3_send.at[peer, side], dst_ref=t3_recv.at[peer, side],
                send_sem=t3_s.at[peer, side], recv_sem=t3_r.at[peer, side],
                device_id={"tp": peer}, device_id_type=MESH).wait_recv()
            total = total + t3_recv[peer, side].astype(F32)
        mq[0, side] = total
        for c in range(n_chip):
            f_send[2 * c + side] = mq[0, side, c * seqs : (c + 1) * seqs, :].astype(BF16)
        for d in range(n_chip):
            to = 2 * lax.rem(chip + d, n_chip) + side
            if d or side is not core:
                pending.append(send(f_send.at[to], f_recv.at[dp], f_s.at[to], f_r.at[dp], {"dp": to}))
            else:
                pltpu.make_async_copy(f_send.at[dp], f_recv.at[dp], loc_sem.at[0]).start()

    project(core)
    for d in range(n_chip):
        recv_g(other, d)
    project(other)
    scatter(core)
    scatter(other)
    pltpu.make_async_copy(f_send.at[dp], f_recv.at[dp], loc_sem.at[0]).wait()
    for d in range(1, n_dp):
        peer = lax.rem(dp + d, n_dp)
        pltpu.make_async_remote_copy(
            src_ref=f_send.at[peer], dst_ref=f_recv.at[peer], send_sem=f_s.at[peer], recv_sem=f_r.at[peer],
            device_id={"dp": peer}, device_id_type=MESH).wait_recv()
    for r in range(n_dp):
        block = slice(r * ocols, (r + 1) * ocols)
        fin[:, block] = fin[:, block] + f_recv[r].astype(F32)
    resid = fin[...]
    inverse = lax.rsqrt(jnp.sum(resid * resid, axis=1, keepdims=True) / width + F32(1e-06))
    weighted = resid * gain[...]
    peak = jnp.max(jnp.abs(weighted), axis=1, keepdims=True)
    scale = (peak * inverse + F32(1e-06)) / F32(448.0)
    scaled = (weighted * (inverse / scale)).astype(BF16)
    for q in range(n_tp):
        o_send[q, 0] = resid[:, q * owide : (q + 1) * owide].astype(BF16)
        o_send[q, 1] = scaled[:, q * owide : (q + 1) * owide]
    spread = jnp.where(lane_i == row_i + tp * seqs, jnp.broadcast_to(scale, lane_i.shape), F32(0.0))
    c_send[...] = jnp.broadcast_to(jnp.sum(spread, axis=0, keepdims=True), c_send.shape)
    for d in range(1, n_tp):
        peer = lax.rem(tp + d, n_tp)
        pending.append(send(c_send, c_recv.at[tp], c_s.at[peer], c_r.at[tp], {"tp": peer}))
    pending += exchange(o_send, o_recv, o_s, o_r, lambda q: None)
    scales = c_send[...]
    for d in range(1, n_tp):
        peer = lax.rem(tp + d, n_tp)
        pltpu.make_async_remote_copy(
            src_ref=c_send, dst_ref=c_recv.at[peer], send_sem=c_s.at[peer], recv_sem=c_r.at[peer],
            device_id={"tp": peer}, device_id_type=MESH).wait_recv()
        scales = scales + c_recv[peer]
    scale_out[...] = scales
    for part, out in ((0, resid_out), (1, scaled_out)):
        for q in range(n_tp):
            b_rows[q * seqs : (q + 1) * seqs, :] = o_recv[q, part].astype(F32)
        out[...] = b_rows[...].astype(BF16)
    for copy in pending:
        copy.wait_send()


def finish(resid, scaled, scale, resid_out, scaled_out, scale_out):
    resid_out[...] = resid[...]
    scaled_out[...] = scaled[...]
    scale_out[...] = scale[0:1, : scale_out.shape[1]]


def fused(n_dp, n_tp, hidden, w_qkv, w_out, norm_gain, kv_cache, lengths):
    rows, width = hidden.shape
    seqs, kvh, ctx, hd2 = kv_cache.shape
    hd = hd2 // 2
    depth, cols = w_qkv.shape
    odepth, ocols = w_out.shape
    heads = odepth * n_tp // hd
    owide = width // n_tp
    chips = n_dp // 2
    vm = pltpu.VMEM
    dma = pltpu.SemaphoreType.DMA
    all_rows = seqs * heads
    scratch = [
        vm((2, chips, rows, depth), BF16), vm((depth, cols), BF16), vm((odepth, ocols), BF16),
        vm(kv_cache.shape, BF16), vm((rows, width), BF16), vm((rows, width), F32),
        vm((chips, rows, cols), BF16), vm((chips, rows, cols), BF16), vm((chips, rows, cols), F32),
        vm((chips, rows, cols), BF16), vm((chips, rows, cols), BF16), vm((rows, cols), F32),
        vm((n_tp, seqs, cols), BF16), vm((n_tp, seqs, cols), BF16),
        vm((all_rows, hd), F32), vm((all_rows, hd), F32), vm((all_rows, hd), F32), vm((all_rows, hd), F32),
        vm((all_rows, ctx), F32), vm((all_rows, hd), F32),
        vm((n_tp, seqs, odepth), BF16), vm((n_tp, seqs, odepth), BF16), vm((rows, odepth), F32),
        vm((2, chips, rows, odepth), BF16), vm((2, chips, rows, ocols), F32),
        vm((n_tp, 2, chips * seqs, ocols), F32), vm((n_tp, 2, chips * seqs, ocols), BF16),
        vm((n_tp, 2, chips * seqs, ocols), BF16),
        vm((n_dp, seqs, ocols), BF16), vm((n_dp, seqs, ocols), BF16),
        vm((n_tp, 2, seqs, owide), BF16), vm((n_tp, 2, seqs, owide), BF16),
        vm((8, hd), F32), vm((n_tp, 8, hd), F32), vm((seqs, width), F32),
        dma((5,)), dma((n_dp,)), dma((n_dp,)), dma, dma, dma((chips,)), dma((chips,)),
        dma((n_tp,)), dma((n_tp,)), dma((n_tp,)), dma((n_tp,)),
        dma((chips,)), dma((2, chips)), dma((chips,)), dma((n_tp, 2)), dma((n_tp, 2)),
        dma((n_dp,)), dma((n_dp,)), dma((n_tp,)), dma((n_tp,)), dma((n_tp,)), dma((n_tp,)),
    ]
    anywhere = pl.BlockSpec(memory_space=pl.ANY)
    in_vmem = pl.BlockSpec(memory_space=pltpu.VMEM)
    resid, scaled, scale = pl.pallas_call(
        functools.partial(layer, n_dp, n_tp),
        out_shape=(
            jax.ShapeDtypeStruct((rows, owide), BF16),
            jax.ShapeDtypeStruct((rows, owide), BF16),
            jax.ShapeDtypeStruct((8, hd), F32),
        ),
        in_specs=[anywhere, anywhere, anywhere, in_vmem, anywhere, pl.BlockSpec(memory_space=pltpu.SMEM)],
        out_specs=(in_vmem, in_vmem, in_vmem),
        scratch_shapes=scratch,
        compiler_params=pltpu.CompilerParams(
            collective_id=0, has_side_effects=True, vmem_limit_bytes=66_000_000),
    )(hidden, w_qkv, w_out, norm_gain.reshape(1, width), kv_cache, lengths)
    resid, scaled, scale = pl.pallas_call(
        finish,
        out_shape=(
            jax.ShapeDtypeStruct((rows, owide), BF16),
            jax.ShapeDtypeStruct((rows, owide), BF16),
            jax.ShapeDtypeStruct((1, rows), F32),
        ),
        in_specs=[in_vmem, in_vmem, in_vmem],
        out_specs=(in_vmem, in_vmem, in_vmem),
    )(resid, scaled, scale)
    return resid, scaled, scale.reshape(rows)


def solution(mesh):
    placed = (
        P("dp", None),
        P("dp", "tp"),
        P("tp", "dp"),
        P(),
        P(("dp", "tp"), None, None, None),
        P(("dp", "tp")),
    )
    n_dp, n_tp = mesh.shape["dp"], mesh.shape["tp"]

    def body(hidden, w_qkv, w_out, norm_gain, kv_cache, lengths):
        lanes = kv_cache.shape[3] // 2
        fits = (
            n_dp % 2 == 0
            and kv_cache.shape[2] == lanes
            and w_qkv.shape[1] % lanes == 0
            and w_out.shape[0] % lanes == 0
            and w_out.shape[1] % lanes == 0
            and hidden.shape[0] <= lanes
            and hidden.shape[1] // n_tp == w_out.shape[0]
        )
        if fits:
            return fused(n_dp, n_tp, hidden, w_qkv, w_out, norm_gain, kv_cache, lengths)
        return shards(hidden, w_qkv, w_out, norm_gain, kv_cache, lengths)

    return jax.shard_map(
        body,
        mesh=mesh,
        in_specs=placed,
        out_specs=(P("dp", "tp"), P("dp", "tp"), P("dp")),
        check_vma=False,
    )
```

profile of v0, /device:TPU:0, one launch (start us, length us, event | category | flops | bytes accessed | tf_op | source)
XLA Modules:
  0.0 61.8 jit_solution(16289963118117226068)
XLA Ops:
  0.6 59.5 %shard_map.85 = (bf16[48,1024]{1,0:T(8,128)(2,1)}, bf16[48,1024]{1,0:T(8,128)(2,1)}, f32[8,128]{1,0:T(8,128)}) custom-call(bf16[48,4096]{1,0:T(8,128)(2,1)} %hidden.1, bf16[512,1152]{1,0:T(8,128)(2,1)} %w_qkv.1, bf16[1024,512]{1,0:T(8,128)(2,1)} %w_out.1, f32[1,4096]{1,0:T(1,128)} %bitcast.2, bf16[12,2,128,256]{3,2,1,0:T(8,128)(2,1)} %cache.1, s32[12]{0:T(128)} %lens.1), custom_call_target="tpu_custom_call" | custom-call | tf_op jit(solution)/shard_map/pallas_call | solution.py:426
  60.1 1.6 %shard_map.86 = (bf16[48,1024]{1,0:T(8,128)(2,1)}, bf16[48,1024]{1,0:T(8,128)(2,1)}, f32[1,48]{1,0:T(1,128)}) custom-call(bf16[48,1024]{1,0:T(8,128)(2,1)} %get-tuple-element.9.resid, bf16[48,1024]{1,0:T(8,128)(2,1)} %get-tuple-element.10.scaled, f32[8,128]{1,0:T(8,128)} %get-tuple-element.11.scale), custom_call_target="tpu_custom_call" | custom-call | tf_op jit(solution)/shard_map/pallas_call | solution.py:439
where the time goes:
time: 62 us; the launch traced here: 61.8 us
  Pallas kernels  61.1 us (99%)
  between operations  0.64 us (1%)
    pallas_call x1, Pallas kernels, fused(): pl.pallas_call(functools.partial(layer, n_dp, n_tp), out_shape=(jax.Shape...  59.5 us
    pallas_call x1, Pallas kernels, fused(): pl.pallas_call(finish, out_shape=(jax.ShapeDtypeStruct((rows, owide), BF1...  1.63 us

commit v1 on v0

v1 whole, which is shorter than its diff:
```python
import functools

import jax
import jax.numpy as jnp
from jax import lax
from jax.experimental import pallas as pl
from jax.experimental.pallas import tpu as pltpu
from jax.sharding import PartitionSpec as P


def rope(values, positions):
    half = values.shape[-1] // 2
    freqs = 1000000.0 ** (-2.0 * jnp.arange(half, dtype=jnp.float32) / values.shape[-1])
    angle = positions[..., None] * freqs
    cosine = jnp.cos(angle)
    sine = jnp.sin(angle)
    first = values[..., :half]
    second = values[..., half:]
    return jnp.concatenate(
        [first * cosine - second * sine, second * cosine + first * sine], axis=-1
    )


def shards(hidden, w_qkv, w_out, norm_gain, kv_cache, lengths):
    seq_dev = kv_cache.shape[0]
    kv_heads = kv_cache.shape[1]
    head_size = kv_cache.shape[3] // 2
    tp_count = lax.axis_size("tp")
    w_cols = lax.all_gather(w_qkv, "dp", axis=0, tiled=True)
    qkv_part = jnp.dot(hidden, w_cols, preferred_element_type=jnp.float32)
    mine = lax.all_to_all(
        qkv_part.astype(jnp.bfloat16), "tp", split_axis=0, concat_axis=1, tiled=True
    )
    att_width = w_out.shape[0] * tp_count
    heads = att_width // head_size
    groups = heads // kv_heads
    positions = lengths.astype(jnp.float32)[:, None]
    query = rope(
        mine[:, :att_width].reshape(seq_dev, heads, head_size).astype(jnp.float32), positions
    ).astype(jnp.bfloat16)
    key_new = rope(
        mine[:, att_width : att_width + kv_heads * head_size]
        .reshape(seq_dev, kv_heads, head_size)
        .astype(jnp.float32),
        positions,
    ).astype(jnp.bfloat16)
    value_new = mine[:, att_width + kv_heads * head_size :].reshape(seq_dev, kv_heads, head_size)
    q_grp = query.reshape(seq_dev, kv_heads, groups, head_size)
    keys = kv_cache[..., :head_size]
    vals = kv_cache[..., head_size:]
    scale = 1.0 / head_size**0.5
    scores = jnp.einsum("nkgd,nkpd->nkgp", q_grp, keys, preferred_element_type=jnp.float32) * scale
    own = jnp.einsum("nkgd,nkd->nkg", q_grp, key_new, preferred_element_type=jnp.float32) * scale
    valid = (jnp.arange(kv_cache.shape[2])[None, :] < lengths[:, None])[:, None, None, :]
    scores = jnp.where(valid, scores, jnp.float32(-1e30))
    top = jnp.maximum(jnp.max(scores, axis=-1), own)
    probs = jnp.where(valid, jnp.exp(scores - top[..., None]), jnp.float32(0.0))
    own_prob = jnp.exp(own - top)
    denom = jnp.sum(probs, axis=-1) + own_prob
    weights = (probs / denom[..., None]).astype(jnp.bfloat16)
    own_weight = (own_prob / denom).astype(jnp.bfloat16)
    mixed = jnp.einsum("nkgp,nkpd->nkgd", weights, vals, preferred_element_type=jnp.float32)
    mixed = (
        mixed
        + own_weight.astype(jnp.float32)[..., None] * value_new.astype(jnp.float32)[:, :, None, :]
    )
    attn = mixed.reshape(seq_dev, att_width).astype(jnp.bfloat16)
    heads_part = lax.all_to_all(attn, "tp", split_axis=1, concat_axis=0, tiled=True)
    terms = jnp.dot(
        heads_part,
        lax.all_gather(w_out, "dp", axis=1, tiled=True),
        preferred_element_type=jnp.float32,
    )
    width = terms.shape[1]
    share = width // tp_count
    offset = lax.axis_index("tp") * share
    summed = lax.psum_scatter(
        terms.astype(jnp.bfloat16), "tp", scatter_dimension=1, tiled=True
    ).astype(jnp.float32)
    hidden_mine = lax.dynamic_slice_in_dim(hidden, offset, share, 1).astype(jnp.float32)
    gain_mine = lax.dynamic_slice_in_dim(norm_gain, offset, share, 0)
    resid_mine = hidden_mine + summed
    weighted = resid_mine * gain_mine[None, :]
    squares = lax.psum(jnp.sum(resid_mine * resid_mine, axis=-1), "tp")
    peak = lax.pmax(jnp.max(jnp.abs(weighted), axis=-1), "tp")
    inverse = lax.rsqrt(squares / width + 1e-06)
    normed_mine = weighted * inverse[:, None]
    row_scale = (peak * inverse + 1e-06) / 448.0
    residual_out = resid_mine.astype(jnp.bfloat16)
    scaled = (normed_mine / row_scale[:, None]).astype(jnp.bfloat16)
    return (residual_out, scaled, row_scale)


F32 = jnp.float32
BF16 = jnp.bfloat16
MESH = pl.DeviceIdType.MESH
VMEM_LIMIT = 66_000_000


def PARTS(seqs):
    return ((0, seqs),)


def send(src, dst, send_sem, recv_sem, where):
    copy = pltpu.make_async_remote_copy(
        src_ref=src, dst_ref=dst, send_sem=send_sem, recv_sem=recv_sem,
        device_id=where, device_id_type=MESH,
    )
    copy.start()
    return copy


def pick(at, table):
    out = jnp.int32(table[0])
    for k in range(1, len(table)):
        out = jnp.where(at == k, jnp.int32(table[k]), out)
    return out


def by_distance(at, count):
    tables = [sorted(range(count), key=lambda k: (abs(k - z), -k if z < count // 2 else k)) for z in range(count)]
    return [pick(at, [tables[z][i] for z in range(count)]) for i in range(count)]


def layer(
    n_dp, n_tp, parts,
    hidden, w_qkv, w_out, gain, cache, lens,
    resid_out, scaled_out, scale_out,
    com, bats,
):
    dp = lax.axis_index("dp")
    tp = lax.axis_index("tp")
    core = lax.rem(dp, 2)
    chip = dp // 2
    partner = chip * 2 + 1 - core
    n_chip = n_dp // 2
    rows = hidden.shape[0]
    seqs = rows // n_tp
    depth = w_qkv.shape[0]
    cols = w_qkv.shape[1]
    ocols = w_out.shape[1]
    owide = resid_out.shape[1]
    kvh = cache.shape[1]
    ctx = cache.shape[2]
    hd = cache.shape[3] // 2
    heads = (w_out.shape[0] * n_tp) // hd
    groups = heads // kvh
    per = cols // hd
    per_out = w_out.shape[0] // hd
    blocks = owide // hd
    width = hidden.shape[1]
    half = hd // 2
    w1, w2, kv, hid, hid32, gmine = (com[k] for k in ("w1", "w2", "kv", "hid", "hid32", "gmine"))
    loc = com["loc"]
    order = by_distance(chip, n_chip)
    peers = [lax.rem(tp + d, n_tp) for d in range(1, n_tp)]

    load_hid = pltpu.make_async_copy(hidden, hid, loc.at[0])
    load_hid.start()
    load_w1 = pltpu.make_async_copy(w_qkv, w1.at[core], loc.at[1])
    load_w1.start()
    load_w2 = pltpu.make_async_copy(w_out, w2.at[core], loc.at[2])
    load_w2.start()
    load_kv = pltpu.make_async_copy(cache, kv, loc.at[3])
    load_kv.start()

    barrier = pltpu.get_barrier_semaphore()
    for d in range(1, n_dp):
        pl.semaphore_signal(barrier, inc=1, device_id={"dp": lax.rem(dp + d, n_dp)}, device_id_type=MESH)
    for d in range(1, n_tp):
        pl.semaphore_signal(barrier, inc=1, device_id={"tp": lax.rem(tp + d, n_tp)}, device_id_type=MESH)

    load_hid.wait()
    hid32[...] = hid[...].astype(F32)
    wide = 2 * depth
    for bat, (first, n) in zip(bats, parts):
        stage = bat["a_stage"]
        for q in range(n_tp):
            stage[q * n : (q + 1) * n, :] = hid32[q * seqs + first : q * seqs + first + n, :]
        for z in range(n_chip):
            bat["a_send"][z] = stage[:, z * wide : (z + 1) * wide].astype(BF16)
    pl.semaphore_wait(barrier, n_dp + n_tp - 2)

    pending = []

    def to(z, q):
        return (z * 2 + core, q)

    def landed(dst, sem):
        pltpu.make_async_remote_copy(
            src_ref=dst, dst_ref=dst, send_sem=sem, recv_sem=sem,
            device_id=(partner, tp), device_id_type=MESH).wait_recv()

    for bat in bats:
        for z in order[1:]:
            pending.append(send(bat["a_send"].at[z], bat["a_recv"].at[chip], bat["a_s"].at[z], bat["a_r"].at[chip], to(z, tp)))
        if bat is bats[0]:
            load_w1.wait()
            swap1 = send(w1.at[core], w1.at[core], com["w_s"].at[0], com["w_r"].at[0], (partner, tp))
            load_w2.wait()
            swap2 = send(w2.at[core], w2.at[core], com["w_s"].at[1], com["w_r"].at[1], (partner, tp))
            pending += [swap1, swap2]

    gmine[...] = gain[:, pl.ds(pl.multiple_of(tp * owide, owide), owide)]
    for bat, (first, n) in zip(bats, parts):
        row_i = lax.broadcasted_iota(jnp.int32, (n, hd), 0)
        lane_i = lax.broadcasted_iota(jnp.int32, (n, hd), 1)
        live = jnp.zeros((n, hd), jnp.int32)
        for s in range(n):
            live = jnp.where(row_i == s, lens[first + s], live)
        low = lane_i < half
        index = jnp.where(low, lane_i, lane_i - half).astype(F32)
        freqs = jnp.exp(index * F32(-2.0 * 13.815510557964274 / hd))
        angle = live.astype(F32) * freqs
        bat["cosine"][...] = jnp.cos(angle)
        bat["sine"][...] = jnp.where(low, -jnp.sin(angle), jnp.sin(angle))
        for h in range(heads):
            bat["l_rows"][pl.ds(h, n, stride=heads), :] = live.astype(F32)
        for z in range(n_chip):
            for j in range(blocks):
                block = slice((z * blocks + j) * hd, (z * blocks + j + 1) * hd)
                mine = bat["a_stage"][0:n, block]
                for q in range(1, n_tp):
                    mine = jnp.where(tp == q, bat["a_stage"][q * n : (q + 1) * n, block], mine)
                bat["hidb"][z, j * n : (j + 1) * n, :] = mine
        if bat["b_stage"].shape[1] > per * n:
            for q in range(n_tp):
                bat["b_stage"][q, per * n :, :] = jnp.zeros((bat["b_stage"].shape[1] - per * n, hd), F32)

    def project_in(b, i):
        bat, (first, n) = bats[b], parts[b]
        z = order[i]
        if i:
            landed(bat["a_recv"].at[z], bat["a_r"].at[z])
            left = bat["a_recv"][z]
        else:
            left = bat["a_send"][chip]
        bat["b_mm"][...] = jnp.dot(left, w1[...].reshape(2 * depth, cols), preferred_element_type=F32)
        for q in range(n_tp):
            for e in range(per):
                bat["b_stage"][q, e * n : (e + 1) * n, :] = bat["b_mm"][q * n : (q + 1) * n, e * hd : (e + 1) * hd]
            bat["b_send"][z, q] = bat["b_stage"][q].astype(BF16)
        for q in ([tp] if i else []) + peers:
            pending.append(send(bat["b_send"].at[z, q], bat["b_recv"].at[chip, tp], bat["b_s"].at[z, q], bat["b_r"].at[chip, tp], to(z, q)))
        if not i:
            bat["b_recv"][chip, tp] = bat["b_send"][chip, tp]

    def attend(b):
        bat, (first, n) = bats[b], parts[b]
        for i, z in enumerate(order):
            for q in ([tp] if i else []) + peers:
                landed(bat["b_recv"].at[z, q], bat["b_r"].at[z, q])
        qkv = bat["qkv"]
        for q in range(n_tp):
            total = bat["b_recv"][0, q].astype(F32)
            for z in range(1, n_chip):
                total = total + bat["b_recv"][z, q].astype(F32)
            qkv[q] = total.astype(BF16).astype(F32)
        cosine = bat["cosine"][...]
        sine = bat["sine"][...]
        q_rows, k_rows, v_rows, s_rows, a_rows = (bat[k] for k in ("q_rows", "k_rows", "v_rows", "s_rows", "a_rows"))

        def head(h):
            return qkv[h // per, (h % per) * n : (h % per + 1) * n, :]

        def turn(x):
            return (x * cosine + pltpu.roll(x, half, 1) * sine).astype(BF16).astype(F32)

        for h in range(heads):
            q_rows[pl.ds(h, n, stride=heads), :] = turn(head(h))
        for k in range(kvh):
            key_new = turn(head(heads + k))
            value_new = head(heads + kvh + k)
            for g in range(groups):
                k_rows[pl.ds(k * groups + g, n, stride=heads), :] = key_new
                v_rows[pl.ds(k * groups + g, n, stride=heads), :] = value_new
        for s in range(n):
            for k in range(kvh):
                at = (s * kvh + k) * groups
                s_rows[at : at + groups, :] = lax.dot_general(
                    q_rows[at : at + groups, :].astype(BF16), kv[first + s, k, :, :hd],
                    (((1,), (1,)), ((), ())), preferred_element_type=F32)
        factor = F32(1.0 / hd**0.5)
        pos = lax.broadcasted_iota(jnp.int32, (n * heads, ctx), 1).astype(F32)
        valid = pos < bat["l_rows"][...]
        scores = jnp.where(valid, s_rows[...] * factor, F32(-1e30))
        own = jnp.sum(q_rows[...] * k_rows[...], axis=1, keepdims=True) * factor
        top = jnp.maximum(jnp.max(scores, axis=1, keepdims=True), own)
        probs = jnp.where(valid, jnp.exp(scores - top), F32(0.0))
        own_prob = jnp.exp(own - top)
        denom = jnp.sum(probs, axis=1, keepdims=True) + own_prob
        s_rows[...] = probs / denom
        own_weight = (own_prob / denom).astype(BF16).astype(F32)
        v_rows[...] = own_weight * v_rows[...]
        for s in range(n):
            for k in range(kvh):
                at = (s * kvh + k) * groups
                a_rows[at : at + groups, :] = jnp.dot(
                    s_rows[at : at + groups, :].astype(BF16), kv[first + s, k, :, hd:],
                    preferred_element_type=F32) + v_rows[at : at + groups, :]
        for q in range(n_tp):
            for e in range(per_out):
                bat["f_stage"][q, e * n : (e + 1) * n, :] = a_rows[pl.ds(q * per_out + e, n, stride=heads), :]
            bat["f_send"][q] = bat["f_stage"][q].astype(BF16)
        for i, z in enumerate(order):
            for q in ([tp] if i else []) + peers:
                pending.append(send(bat["f_send"].at[q], bat["f_recv"].at[chip, tp], bat["f_s"].at[z, q], bat["f_r"].at[chip, tp], to(z, q)))
        bat["f_recv"][chip, tp] = bat["f_send"][tp]

    def project_out(b, i):
        bat, (first, n) = bats[b], parts[b]
        z = order[i]
        for q in ([tp] if i else []) + peers:
            landed(bat["f_recv"].at[z, q], bat["f_r"].at[z, q])
        for q in range(n_tp):
            bat["f_stage"][q] = bat["f_recv"][z, q].astype(F32)
            for e in range(per_out):
                bat["o_left"][q * n : (q + 1) * n, e * hd : (e + 1) * hd] = bat["f_stage"][q, e * n : (e + 1) * n, :]
        left = bat["o_left"][...].astype(BF16)
        for c in range(2):
            bat["o_mm"][:, c * ocols : (c + 1) * ocols] = jnp.dot(left, w2[c], preferred_element_type=F32)
        for q in range(n_tp):
            for j in range(blocks):
                bat["g_stage"][q, j * n : (j + 1) * n, :] = bat["o_mm"][q * n : (q + 1) * n, j * hd : (j + 1) * hd]
            bat["g_send"][z, q] = bat["g_stage"][q].astype(BF16)
        for q in peers:
            pending.append(send(bat["g_send"].at[z, q], bat["g_recv"].at[z, tp], bat["g_s"].at[z, q], bat["g_r"].at[z, tp], to(chip, q)))

    def add_up(b, i):
        bat = bats[b]
        z = order[i]
        total = bat["g_send"][z, tp].astype(F32)
        for q in peers:
            landed(bat["g_recv"].at[z, q], bat["g_r"].at[z, q])
            total = total + bat["g_recv"][z, q].astype(F32)
        if i:
            bat["h_send"][z] = total.astype(BF16)
            pending.append(send(bat["h_send"].at[z], bat["h_recv"].at[chip], bat["h_s"].at[z], bat["h_r"].at[chip], to(z, tp)))
        else:
            bat["h_recv"][chip] = total.astype(BF16)

    def norm(b):
        bat, (first, n) = bats[b], parts[b]
        for z in order[1:]:
            landed(bat["h_recv"].at[z], bat["h_r"].at[z])
        squares = jnp.zeros((n, hd), F32)
        peak = jnp.zeros((n, hd), F32)
        resid = bat["resid"]
        for z in range(n_chip):
            resid[z] = bat["h_recv"][z].astype(F32) + bat["hidb"][z]
            bat["j_send"][z] = resid[z].astype(BF16)
        for q in peers:
            pending.append(send(bat["j_send"].at[q], bat["j_recv"].at[tp], bat["j_s"].at[q], bat["j_r"].at[tp], to(chip, q)))
        for z in range(n_chip):
            for j in range(blocks):
                part = resid[z, j * n : (j + 1) * n, :]
                squares = squares + part * part
                at = (z * blocks + j) * hd
                peak = jnp.maximum(peak, jnp.abs(part * gain[:, at : at + hd]))
        inverse = lax.rsqrt(jnp.sum(squares, axis=1, keepdims=True) / width + F32(1e-06))
        scale = (jnp.max(peak, axis=1, keepdims=True) * inverse + F32(1e-06)) / F32(448.0)
        lane_i = lax.broadcasted_iota(jnp.int32, (n, hd), 1)
        bat["c_send"][...] = jnp.where(lane_i < half, inverse / scale, scale)
        for q in peers:
            pending.append(send(bat["c_send"], bat["c_recv"].at[tp], bat["c_s"].at[q], bat["c_r"].at[tp], to(chip, q)))
        bat["j_recv"][tp] = bat["j_send"][tp]
        bat["c_recv"][tp] = bat["c_send"][...]

    def finish_rows(b, scales):
        bat, (first, n) = bats[b], parts[b]
        for q in peers:
            landed(bat["c_recv"].at[q], bat["c_r"].at[q])
            landed(bat["j_recv"].at[q], bat["j_r"].at[q])
        row_i = lax.broadcasted_iota(jnp.int32, (n, hd), 0)
        lane_i = lax.broadcasted_iota(jnp.int32, (n, hd), 1)
        for q in range(n_tp):
            bat["resid"][q] = bat["j_recv"][q].astype(F32)
            stats = bat["c_recv"][q]
            factor = jnp.broadcast_to(stats[:, 0:1], (n, hd))
            scale = jnp.broadcast_to(stats[:, half : half + 1], (n, hd))
            spread = jnp.where(lane_i == row_i + (q * seqs + first), scale, F32(0.0))
            scales = scales + jnp.sum(spread, axis=0, keepdims=True)
            at = slice(q * seqs + first, q * seqs + first + n)
            for j in range(blocks):
                block = slice(j * hd, (j + 1) * hd)
                part = bat["resid"][q, j * n : (j + 1) * n, :]
                com["r_out"][at, block] = part
                com["x_out"][at, block] = part * gmine[:, block] * factor
        return scales

    count = len(parts)
    for b in range(count):
        for i in range(n_chip):
            if b == 0 and i == 0:
                swap1.wait_recv()
            project_in(b, i)
    load_kv.wait()
    for b in range(count):
        attend(b)
    swap2.wait_recv()
    for b in range(count):
        for i in range(n_chip):
            project_out(b, i)
            if i:
                add_up(b, i - 1)
        add_up(b, n_chip - 1)
    for b in range(count):
        norm(b)
    scales = jnp.zeros((1, hd), F32)
    for b in range(count):
        scales = finish_rows(b, scales)
    scale_out[...] = jnp.broadcast_to(scales, scale_out.shape)
    resid_out[...] = com["r_out"][...].astype(BF16)
    scaled_out[...] = com["x_out"][...].astype(BF16)
    for copy in pending:
        copy.wait_send()


def finish(resid, scaled, scale, resid_out, scaled_out, scale_out):
    resid_out[...] = resid[...]
    scaled_out[...] = scaled[...]
    scale_out[...] = scale[0:1, : scale_out.shape[1]]


def fused(n_dp, n_tp, hidden, w_qkv, w_out, norm_gain, kv_cache, lengths):
    rows, width = hidden.shape
    seqs, kvh, ctx, hd2 = kv_cache.shape
    hd = hd2 // 2
    depth, cols = w_qkv.shape
    odepth, ocols = w_out.shape
    heads = odepth * n_tp // hd
    owide = width // n_tp
    chips = n_dp // 2
    per, per_out, blocks = cols // hd, odepth // hd, owide // hd
    vm = pltpu.VMEM
    dma = pltpu.SemaphoreType.DMA
    parts = PARTS(seqs)
    com = dict(
        w1=vm((2, depth, cols), BF16), w2=vm((2, odepth, ocols), BF16), kv=vm(kv_cache.shape, BF16),
        hid=vm((rows, width), BF16), hid32=vm((rows, width), F32), gmine=vm((1, owide), F32),
        r_out=vm((rows, owide), F32), x_out=vm((rows, owide), F32),
        loc=dma((4,)), w_s=dma((2,)), w_r=dma((2,)),
    )
    bats = []
    for _, n in parts:
        pad = -(-per * n // 16) * 16
        bats.append(dict(
            a_stage=vm((n_tp * n, width), F32), a_send=vm((chips, n_tp * n, 2 * depth), BF16),
            a_recv=vm((chips, n_tp * n, 2 * depth), BF16), hidb=vm((chips, blocks * n, hd), F32),
            b_mm=vm((n_tp * n, cols), F32), b_stage=vm((n_tp, pad, hd), F32),
            b_send=vm((chips, n_tp, pad, hd), BF16), b_recv=vm((chips, n_tp, pad, hd), BF16),
            qkv=vm((n_tp, pad, hd), F32), cosine=vm((n, hd), F32), sine=vm((n, hd), F32),
            q_rows=vm((n * heads, hd), F32), k_rows=vm((n * heads, hd), F32), v_rows=vm((n * heads, hd), F32),
            l_rows=vm((n * heads, hd), F32), s_rows=vm((n * heads, ctx), F32), a_rows=vm((n * heads, hd), F32),
            f_stage=vm((n_tp, per_out * n, hd), F32), f_send=vm((n_tp, per_out * n, hd), BF16),
            f_recv=vm((chips, n_tp, per_out * n, hd), BF16),
            o_left=vm((n_tp * n, odepth), F32), o_mm=vm((n_tp * n, owide), F32),
            g_stage=vm((n_tp, blocks * n, hd), F32), g_send=vm((chips, n_tp, blocks * n, hd), BF16),
            g_recv=vm((chips, n_tp, blocks * n, hd), BF16),
            h_send=vm((chips, blocks * n, hd), BF16), h_recv=vm((chips, blocks * n, hd), BF16),
            resid=vm((chips, blocks * n, hd), F32),
            j_send=vm((chips, blocks * n, hd), BF16), j_recv=vm((n_tp, blocks * n, hd), BF16),
            c_send=vm((n, hd), F32), c_recv=vm((n_tp, n, hd), F32),
            a_s=dma((chips,)), a_r=dma((chips,)), b_s=dma((chips, n_tp)), b_r=dma((chips, n_tp)),
            f_s=dma((chips, n_tp)), f_r=dma((chips, n_tp)), g_s=dma((chips, n_tp)), g_r=dma((chips, n_tp)),
            h_s=dma((chips,)), h_r=dma((chips,)), j_s=dma((n_tp,)), j_r=dma((n_tp,)), c_s=dma((n_tp,)), c_r=dma((n_tp,)),
        ))
    anywhere = pl.BlockSpec(memory_space=pl.ANY)
    in_vmem = pl.BlockSpec(memory_space=pltpu.VMEM)
    resid, scaled, scale = pl.pallas_call(
        functools.partial(layer, n_dp, n_tp, parts),
        out_shape=(
            jax.ShapeDtypeStruct((rows, owide), BF16),
            jax.ShapeDtypeStruct((rows, owide), BF16),
            jax.ShapeDtypeStruct((8, hd), F32),
        ),
        in_specs=[anywhere, anywhere, anywhere, in_vmem, anywhere, pl.BlockSpec(memory_space=pltpu.SMEM)],
        out_specs=(in_vmem, in_vmem, in_vmem),
        scratch_shapes=[com, bats],
        compiler_params=pltpu.CompilerParams(
            collective_id=0, has_side_effects=True, vmem_limit_bytes=VMEM_LIMIT),
    )(hidden, w_qkv, w_out, norm_gain.reshape(1, width), kv_cache, lengths)
    resid, scaled, scale = pl.pallas_call(
        finish,
        out_shape=(
            jax.ShapeDtypeStruct((rows, owide), BF16),
            jax.ShapeDtypeStruct((rows, owide), BF16),
            jax.ShapeDtypeStruct((1, rows), F32),
        ),
        in_specs=[in_vmem, in_vmem, in_vmem],
        out_specs=(in_vmem, in_vmem, in_vmem),
    )(resid, scaled, scale)
    return resid, scaled, scale.reshape(rows)


def solution(mesh):
    placed = (
        P("dp", None),
        P("dp", "tp"),
        P("tp", "dp"),
        P(),
        P(("dp", "tp"), None, None, None),
        P(("dp", "tp")),
    )
    n_dp, n_tp = mesh.shape["dp"], mesh.shape["tp"]

    def body(hidden, w_qkv, w_out, norm_gain, kv_cache, lengths):
        lanes = kv_cache.shape[3] // 2
        fits = (
            n_dp % 2 == 0
            and kv_cache.shape[2] == lanes
            and w_qkv.shape[1] % lanes == 0
            and w_out.shape[0] % lanes == 0
            and w_out.shape[1] % lanes == 0
            and hidden.shape[0] <= lanes
            and hidden.shape[1] // n_tp == w_out.shape[0]
            and n_dp == 2 * n_tp
            and hidden.shape[1] == n_dp * w_out.shape[1]
            and hidden.shape[1] == n_dp * w_qkv.shape[0]
        )
        if fits:
            return fused(n_dp, n_tp, hidden, w_qkv, w_out, norm_gain, kv_cache, lengths)
        return shards(hidden, w_qkv, w_out, norm_gain, kv_cache, lengths)

    return jax.shard_map(
        body,
        mesh=mesh,
        in_specs=placed,
        out_specs=(P("dp", "tp"), P("dp", "tp"), P("dp")),
        check_vma=False,
    )
```

time: 62 us -> 54.3 us (0.88)
  Pallas kernels: 61.1 us -> 53.4 us
    pallas_call x1, Pallas kernels: 59.5 us -> 51.8 us  [fused(): pl.pallas_call(functools.partial(layer, n_dp, n_tp, parts), out_shape=(ja...]
where the time goes in v1:
time: 54.3 us; the launch traced here: 54 us
  Pallas kernels  53.4 us (98%)
  between operations  0.64 us (1%)
    pallas_call x1, Pallas kernels, fused(): pl.pallas_call(functools.partial(layer, n_dp, n_tp, parts), out_shape=(ja...  51.8 us
    pallas_call x1, Pallas kernels, fused(): pl.pallas_call(finish, out_shape=(jax.ShapeDtypeStruct((rows, owide), BF1...  1.63 us

profile of v1, /device:TPU:0, one launch (start us, length us, event | category | flops | bytes accessed | tf_op | source)
XLA Modules:
  0.0 54.0 jit_solution(12437977732704262844)
XLA Ops:
  0.6 51.8 %shard_map.85 = (bf16[48,1024]{1,0:T(8,128)(2,1)}, bf16[48,1024]{1,0:T(8,128)(2,1)}, f32[8,128]{1,0:T(8,128)}) custom-call(bf16[48,4096]{1,0:T(8,128)(2,1)} %hidden.1, bf16[512,1152]{1,0:T(8,128)(2,1)} %w_qkv.1, bf16[1024,512]{1,0:T(8,128)(2,1)} %w_out.1, f32[1,4096]{1,0:T(1,128)} %bitcast.2, bf16[12,2,128,256]{3,2,1,0:T(8,128)(2,1)} %cache.1, s32[12]{0:T(128)} %lens.1), custom_call_target="tpu_custom_call" | custom-call | tf_op jit(solution)/shard_map/pallas_call | solution.py:470
  52.4 1.6 %shard_map.86 = (bf16[48,1024]{1,0:T(8,128)(2,1)}, bf16[48,1024]{1,0:T(8,128)(2,1)}, f32[1,48]{1,0:T(1,128)}) custom-call(bf16[48,1024]{1,0:T(8,128)(2,1)} %get-tuple-element.9.resid, bf16[48,1024]{1,0:T(8,128)(2,1)} %get-tuple-element.10.scaled, f32[8,128]{1,0:T(8,128)} %get-tuple-element.11.scale), custom_call_target="tpu_custom_call" | custom-call | tf_op jit(solution)/shard_map/pallas_call | solution.py:483

commit v2 on v1

--- a/solution.py
+++ b/solution.py
@@ -94,7 +94,7 @@
 F32 = jnp.float32
 BF16 = jnp.bfloat16
 MESH = pl.DeviceIdType.MESH
-VMEM_LIMIT = 66_000_000
+VMEM_LIMIT = 56_300_000
 
 
 def PARTS(seqs):
@@ -117,14 +117,18 @@
     return out
 
 
-def by_distance(at, count):
-    tables = [sorted(range(count), key=lambda k: (abs(k - z), -k if z < count // 2 else k)) for z in range(count)]
-    return [pick(at, [tables[z][i] for z in range(count)]) for i in range(count)]
+def chip_order(at, count):
+    tables = []
+    for z in range(count):
+        others = sorted((k for k in range(count) if k != z), key=lambda k: (abs(k - z) == 2, abs(k - z), -k if z < count // 2 else k))
+        tables.append([z] + others)
+    spread = all(sum(abs(k - z) == 2 for k in range(count)) == 1 for z in range(count))
+    return [pick(at, [tables[z][i] for z in range(count)]) for i in range(count)], spread
 
 
 def layer(
     n_dp, n_tp, parts,
-    hidden, w_qkv, w_out, gain, cache, lens,
+    hidden, w_qkv, w_out, gain_in, cache, lens_in,
     resid_out, scaled_out, scale_out,
     com, bats,
 ):
@@ -150,9 +154,11 @@
     blocks = owide // hd
     width = hidden.shape[1]
     half = hd // 2
-    w1, w2, kv, hid, hid32, gmine = (com[k] for k in ("w1", "w2", "kv", "hid", "hid32", "gmine"))
+    w1, w2, kv, hid, hid32, gain, gmine, lens = (
+        com[k] for k in ("w1", "w2", "kv", "hid", "hid32", "gain", "gmine", "lens"))
     loc = com["loc"]
-    order = by_distance(chip, n_chip)
+    order, spread = chip_order(chip, n_chip)
+    direct = order[1:-1] if spread else order[1:]
     peers = [lax.rem(tp + d, n_tp) for d in range(1, n_tp)]
 
     load_hid = pltpu.make_async_copy(hidden, hid, loc.at[0])
@@ -163,6 +169,10 @@
     load_w2.start()
     load_kv = pltpu.make_async_copy(cache, kv, loc.at[3])
     load_kv.start()
+    load_gain = pltpu.make_async_copy(gain_in, gain, loc.at[4])
+    load_gain.start()
+    load_lens = pltpu.make_async_copy(lens_in, lens, loc.at[5])
+    load_lens.start()
 
     barrier = pltpu.get_barrier_semaphore()
     for d in range(1, n_dp):
@@ -171,14 +181,22 @@
         pl.semaphore_signal(barrier, inc=1, device_id={"tp": lax.rem(tp + d, n_tp)}, device_id_type=MESH)
 
     load_hid.wait()
+    wide = 2 * depth
+
+    def own_part(z):
+        return hid.at[:, pl.ds(pl.multiple_of(z * wide, wide), wide)]
+
     hid32[...] = hid[...].astype(F32)
-    wide = 2 * depth
     for bat, (first, n) in zip(bats, parts):
-        stage = bat["a_stage"]
-        for q in range(n_tp):
-            stage[q * n : (q + 1) * n, :] = hid32[q * seqs + first : q * seqs + first + n, :]
         for z in range(n_chip):
-            bat["a_send"][z] = stage[:, z * wide : (z + 1) * wide].astype(BF16)
+            for j in range(blocks):
+                block = slice((z * blocks + j) * hd, (z * blocks + j + 1) * hd)
+                mine = hid32[first : first + n, block]
+                for q in range(1, n_tp):
+                    mine = jnp.where(tp == q, hid32[q * seqs + first : q * seqs + first + n, block], mine)
+                bat["hidb"][z, j * n : (j + 1) * n, :] = mine
+        if spread:
+            bat["a2_send"][...] = bat["hidb"][order[-1]].astype(BF16)
     pl.semaphore_wait(barrier, n_dp + n_tp - 2)
 
     pending = []
@@ -192,15 +210,18 @@
             device_id=(partner, tp), device_id_type=MESH).wait_recv()
 
     for bat in bats:
-        for z in order[1:]:
-            pending.append(send(bat["a_send"].at[z], bat["a_recv"].at[chip], bat["a_s"].at[z], bat["a_r"].at[chip], to(z, tp)))
-        if bat is bats[0]:
-            load_w1.wait()
-            swap1 = send(w1.at[core], w1.at[core], com["w_s"].at[0], com["w_r"].at[0], (partner, tp))
-            load_w2.wait()
-            swap2 = send(w2.at[core], w2.at[core], com["w_s"].at[1], com["w_r"].at[1], (partner, tp))
-            pending += [swap1, swap2]
-
+        if spread:
+            pending.append(send(bat["a2_send"], bat["a2_recv"].at[tp], bat["a2_s"].at[tp], bat["a2_r"].at[tp], to(order[-1], tp)))
+        for z in direct:
+            pending.append(send(own_part(z), bat["a_recv"].at[chip], bat["a_s"].at[z], bat["a_r"].at[chip], to(z, tp)))
+    load_w1.wait()
+    swap1 = send(w1.at[core], w1.at[core], com["w_s"].at[0], com["w_r"].at[0], (partner, tp))
+    load_w2.wait()
+    swap2 = send(w2.at[core], w2.at[core], com["w_s"].at[1], com["w_r"].at[1], (partner, tp))
+    pending += [swap1, swap2]
+
+    load_lens.wait()
+    load_gain.wait()
     gmine[...] = gain[:, pl.ds(pl.multiple_of(tp * owide, owide), owide)]
     for bat, (first, n) in zip(bats, parts):
         row_i = lax.broadcasted_iota(jnp.int32, (n, hd), 0)
@@ -216,25 +237,32 @@
         bat["sine"][...] = jnp.where(low, -jnp.sin(angle), jnp.sin(angle))
         for h in range(heads):
             bat["l_rows"][pl.ds(h, n, stride=heads), :] = live.astype(F32)
-        for z in range(n_chip):
-            for j in range(blocks):
-                block = slice((z * blocks + j) * hd, (z * blocks + j + 1) * hd)
-                mine = bat["a_stage"][0:n, block]
-                for q in range(1, n_tp):
-                    mine = jnp.where(tp == q, bat["a_stage"][q * n : (q + 1) * n, block], mine)
-                bat["hidb"][z, j * n : (j + 1) * n, :] = mine
         if bat["b_stage"].shape[1] > per * n:
             for q in range(n_tp):
                 bat["b_stage"][q, per * n :, :] = jnp.zeros((bat["b_stage"].shape[1] - per * n, hd), F32)
 
+    def spread_a(b):
+        bat = bats[b]
+        landed(bat["a2_recv"].at[tp], bat["a2_r"].at[tp])
+        for q in peers:
+            pending.append(send(bat["a2_recv"].at[tp], bat["a2_recv"].at[tp], bat["a2_s"].at[q], bat["a2_r"].at[tp], to(chip, q)))
+
     def project_in(b, i):
         bat, (first, n) = bats[b], parts[b]
         z = order[i]
-        if i:
+        if not i:
+            left = own_part(chip)[...]
+        elif spread and i == n_chip - 1:
+            for q in peers:
+                landed(bat["a2_recv"].at[q], bat["a2_r"].at[q])
+            for q in range(n_tp):
+                bat["f_stage"][q] = bat["a2_recv"][q].astype(F32)
+                for j in range(blocks):
+                    bat["a_left"][q * n : (q + 1) * n, j * hd : (j + 1) * hd] = bat["f_stage"][q, j * n : (j + 1) * n, :]
+            left = bat["a_left"][...].astype(BF16)
+        else:
             landed(bat["a_recv"].at[z], bat["a_r"].at[z])
             left = bat["a_recv"][z]
-        else:
-            left = bat["a_send"][chip]
         bat["b_mm"][...] = jnp.dot(left, w1[...].reshape(2 * depth, cols), preferred_element_type=F32)
         for q in range(n_tp):
             for e in range(per):
@@ -394,6 +422,8 @@
             if b == 0 and i == 0:
                 swap1.wait_recv()
             project_in(b, i)
+            if spread and i == 0:
+                spread_a(b)
     load_kv.wait()
     for b in range(count):
         attend(b)
@@ -437,15 +467,17 @@
     parts = PARTS(seqs)
     com = dict(
         w1=vm((2, depth, cols), BF16), w2=vm((2, odepth, ocols), BF16), kv=vm(kv_cache.shape, BF16),
-        hid=vm((rows, width), BF16), hid32=vm((rows, width), F32), gmine=vm((1, owide), F32),
+        hid=vm((rows, width), BF16), hid32=vm((rows, width), F32), gain=vm((1, width), F32), gmine=vm((1, owide), F32),
+        lens=pltpu.SMEM((seqs,), jnp.int32),
         r_out=vm((rows, owide), F32), x_out=vm((rows, owide), F32),
-        loc=dma((4,)), w_s=dma((2,)), w_r=dma((2,)),
+        loc=dma((6,)), w_s=dma((2,)), w_r=dma((2,)),
     )
     bats = []
     for _, n in parts:
         pad = -(-per * n // 16) * 16
         bats.append(dict(
-            a_stage=vm((n_tp * n, width), F32), a_send=vm((chips, n_tp * n, 2 * depth), BF16),
+            a2_send=vm((blocks * n, hd), BF16), a2_recv=vm((n_tp, blocks * n, hd), BF16),
+            a_left=vm((n_tp * n, 2 * depth), F32), a2_s=dma((n_tp,)), a2_r=dma((n_tp,)),
             a_recv=vm((chips, n_tp * n, 2 * depth), BF16), hidb=vm((chips, blocks * n, hd), F32),
             b_mm=vm((n_tp * n, cols), F32), b_stage=vm((n_tp, pad, hd), F32),
             b_send=vm((chips, n_tp, pad, hd), BF16), b_recv=vm((chips, n_tp, pad, hd), BF16),
@@ -465,7 +497,7 @@
             f_s=dma((chips, n_tp)), f_r=dma((chips, n_tp)), g_s=dma((chips, n_tp)), g_r=dma((chips, n_tp)),
             h_s=dma((chips,)), h_r=dma((chips,)), j_s=dma((n_tp,)), j_r=dma((n_tp,)), c_s=dma((n_tp,)), c_r=dma((n_tp,)),
         ))
-    anywhere = pl.BlockSpec(memory_space=pl.ANY)
+    in_hbm = pl.BlockSpec(memory_space=pltpu.HBM)
     in_vmem = pl.BlockSpec(memory_space=pltpu.VMEM)
     resid, scaled, scale = pl.pallas_call(
         functools.partial(layer, n_dp, n_tp, parts),
@@ -474,7 +506,7 @@
             jax.ShapeDtypeStruct((rows, owide), BF16),
             jax.ShapeDtypeStruct((8, hd), F32),
         ),
-        in_specs=[anywhere, anywhere, anywhere, in_vmem, anywhere, pl.BlockSpec(memory_space=pltpu.SMEM)],
+        in_specs=[in_hbm] * 6,
         out_specs=(in_vmem, in_vmem, in_vmem),
         scratch_shapes=[com, bats],
         compiler_params=pltpu.CompilerParams(
@@ -489,6 +521,7 @@
         ),
         in_specs=[in_vmem, in_vmem, in_vmem],
         out_specs=(in_vmem, in_vmem, in_vmem),
+        compiler_params=pltpu.CompilerParams(vmem_limit_bytes=2_000_000),
     )(resid, scaled, scale)
     return resid, scaled, scale.reshape(rows)
 

time: 54.3 us -> 50.5 us (0.930)
  Pallas kernels: 53.4 us -> 48.3 us
  local copies, waits for them, and re-layouts: 0 us -> 1.37 us
    pallas_call x1, Pallas kernels: 51.8 us -> 47.6 us  [fused(): pl.pallas_call(functools.partial(layer, n_dp, n_tp, parts), out_shape=(ja...]
    unnamed x0 -> x4, local copies, waits for them, and re-layouts: none -> 1.37 us
    pallas_call x1, Pallas kernels: 1.63 us -> 0.69 us  [fused(): pl.pallas_call(finish, out_shape=(jax.ShapeDtypeStruct((rows, owide), BF1...]
where the time goes in v2:
time: 50.5 us; the launch traced here: 50.3 us
  Pallas kernels  48.3 us (96%)
  local copies, waits for them, and re-layouts  1.37 us (3%)
  between operations  0.65 us (1%)
    pallas_call x1, Pallas kernels, fused(): pl.pallas_call(functools.partial(layer, n_dp, n_tp, parts), out_shape=(ja...  47.6 us
    unnamed x4, local copies, waits for them, and re-layouts  1.37 us

profile of v2, /device:TPU:0, one launch (start us, length us, event | category | flops | bytes accessed | tf_op | source)
XLA Modules:
  0.0 50.3 jit_solution(7313210782205149233)
XLA Ops:
  0.6 0.0 copy-start
  0.6 0.7 %copy-done = f32[4096]{0:T(1024)S(1)} copy-done((f32[4096]{0:T(1024)S(1)}, f32[4096]{0:T(1024)}, u32[]{:S(2)}) %copy-start) | copy-done | bytes 16408
  1.4 0.0 copy-start.1
  1.4 0.7 %copy-done.1 = s32[12]{0:T(128)S(1)} copy-done((s32[12]{0:T(128)S(1)}, s32[12]{0:T(128)}, u32[]{:S(2)}) %copy-start.1) | copy-done | bytes 72
  2.0 47.6 %shard_map.85 = (bf16[48,1024]{1,0:T(8,128)(2,1)S(1)}, bf16[48,1024]{1,0:T(8,128)(2,1)S(1)}, f32[8,128]{1,0:T(8,128)S(1)}) custom-call(bf16[48,4096]{1,0:T(8,128)(2,1)} %hidden.1, bf16[512,1152]{1,0:T(8,128)(2,1)} %w_qkv.1, bf16[1024,512]{1,0:T(8,128)(2,1)} %w_out.1, f32[1,4096]{1,0:T(1,128)S(1)} %bitcast.2, bf16[12,2,128,256]{3,2,1,0:T(8,128)(2,1)} %cache.1, ...), custom_call_target="tpu_custom_call" | custom-call | tf_op jit(solution)/shard_map/pallas_call | solution.py:502
  49.6 0.7 %shard_map.86 = (bf16[48,1024]{1,0:T(8,128)(2,1)}, bf16[48,1024]{1,0:T(8,128)(2,1)}, f32[1,48]{1,0:T(1,128)}) custom-call(bf16[48,1024]{1,0:T(8,128)(2,1)S(1)} %get-tuple-element.9.resid, bf16[48,1024]{1,0:T(8,128)(2,1)S(1)} %get-tuple-element.10.scaled, f32[8,128]{1,0:T(8,128)S(1)} %get-tuple-element.11.scale), custom_call_target="tpu_custom_call" | custom-call | tf_op jit(solution)/shard_map/pallas_call | solution.py:515
Async XLA Ops:
  0.6 0.7 %copy-start = (f32[4096]{0:T(1024)S(1)}, f32[4096]{0:T(1024)}, u32[]{:S(2)}) copy-start(f32[4096]{0:T(1024)} %param.9) | copy-start | bytes 49156
  1.4 0.7 %copy-start.1 = (s32[12]{0:T(128)S(1)}, s32[12]{0:T(128)}, u32[]{:S(2)}) copy-start(s32[12]{0:T(128)} %lens_in.1) | copy-start | bytes 148
